TPU v7x, 32 devices: a whole 2x2x4 slice. The times are simulated.
32 devices in a mesh: fsdp: 16 (over z, x, core), tp: 2 (over y).
Axes of the slice: x: 2, y: 2, z: 4, core: 2. Of those that a mesh axis runs over, the one named last changes fastest.
Arguments:
- inputs: bfloat16 [32768, 1024], P(('fsdp', 'tp')), may hold values from -6 to 6
- cotangent: bfloat16 [32768, 1024], P(('fsdp', 'tp')), may hold values from -18 to 18
- first_gain: float32 [1024], replicated, may hold values from 0.5 to 1.5
- first_shift: float32 [1024], replicated, may hold values from -1.5 to 1.5
- second_gain: float32 [1024], replicated, may hold values from 0.5 to 1.5
- second_shift: float32 [1024], replicated, may hold values from -1.5 to 1.5
- project_weight: bfloat16 [1024, 3, 1024], P('fsdp', None, 'tp'), may hold values from -0.1875 to 0.1875
- project_bias: float32 [3, 1024], P(None, 'tp'), may hold values from -1.5 to 1.5
- dense_weight: bfloat16 [1024, 1024], P('tp', 'fsdp'), may hold values from -4 to 4
- dense_bias: float32 [1024], replicated, may hold values from -1.5 to 1.5
- expand_weight: bfloat16 [1024, 4096], P('fsdp', 'tp'), may hold values from -0.1875 to 0.1875
- expand_bias: float32 [4096], P('tp'), may hold values from -2.5 to 2.5
- shrink_weight: bfloat16 [4096, 1024], P('tp', 'fsdp'), may hold values from -0.09375 to 0.09375
- shrink_bias: float32 [1024], replicated, may hold values from -1.5 to 1.5
Outputs:
- output: bfloat16 [32768, 1024], P(('fsdp', 'tp'))
- input_grad: float32 [32768, 1024], P(('fsdp', 'tp'))
- first_gain_grad: float32 [1024], replicated
- first_shift_grad: float32 [1024], replicated
- second_gain_grad: float32 [1024], replicated
- second_shift_grad: float32 [1024], replicated
- project_weight_grad: float32 [1024, 3, 1024], P('fsdp', None, 'tp')
- project_bias_grad: float32 [3, 1024], P(None, 'tp')
- dense_weight_grad: float32 [1024, 1024], P('tp', 'fsdp')
- dense_bias_grad: float32 [1024], replicated
- expand_weight_grad: float32 [1024, 4096], P('fsdp', 'tp')
- expand_bias_grad: float32 [4096], P('tp')
- shrink_weight_grad: float32 [4096, 1024], P('tp', 'fsdp')
- shrink_bias_grad: float32 [1024], replicated
All inputs are finite; a program needn't handle non-finite values.
Results may differ from a plain program's by a relative error of at most 0.0094.
Values may be sent and summed in bfloat16 or wider, within the bound.
A program may use at most 320 MiB of HBM per device.

v0:
```python
import jax
import jax.numpy as jnp
from jax import lax
from jax.sharding import PartitionSpec as P

HS = 64
ROT = 16
LEN = 2048
EPS = 1e-05


def normalize(values, gain_vector, shift_vector):
    mean_row = jnp.mean(values, axis=-1, keepdims=True)
    centred = values - mean_row
    spread = lax.rsqrt(jnp.mean(centred * centred, axis=-1, keepdims=True) + EPS)
    normal = centred * spread
    return (normal * gain_vector + shift_vector, normal, spread)


def norm_back(grad_in, normal, spread, gain_vector):
    scaled = grad_in * gain_vector
    mean_first = jnp.mean(scaled, axis=-1, keepdims=True)
    mean_second = jnp.mean(scaled * normal, axis=-1, keepdims=True)
    return spread * (scaled - mean_first - normal * mean_second)


def rotary_tables(row_count):
    half_rot = ROT // 2
    position = (jnp.arange(row_count) % LEN).astype(jnp.float32)
    inverse = 10000.0 ** (-(jnp.arange(half_rot).astype(jnp.float32) * 2.0) / ROT)
    angle = position[:, None] * inverse[None, :]
    return (jnp.cos(angle), jnp.sin(angle))


def rotate(heads_in, cosine_table, sine_table):
    half_rot = ROT // 2
    first_half = heads_in[..., :half_rot]
    second_half = heads_in[..., half_rot:ROT]
    cos_wide = cosine_table[:, None, :]
    sin_wide = sine_table[:, None, :]
    return jnp.concatenate(
        [
            first_half * cos_wide - second_half * sin_wide,
            second_half * cos_wide + first_half * sin_wide,
            heads_in[..., ROT:],
        ],
        axis=-1,
    )


def causal_scores(query_rows, key_rows, first_row, score_scale):
    block_rows = query_rows.shape[0]
    raw_scores = (
        jnp.einsum("qhd,khd->hqk", query_rows, key_rows, preferred_element_type=jnp.float32)
        * score_scale
    )
    row_pos = first_row + jnp.arange(block_rows)[:, None]
    col_pos = jnp.arange(key_rows.shape[0])[None, :]
    return jnp.where((col_pos <= row_pos)[None], raw_scores, -1e30)


def gelu_exact(pre_act):
    return jax.nn.gelu(pre_act, approximate=False)


def body(
    inputs,
    cotangent,
    first_gain,
    first_shift,
    second_gain,
    second_shift,
    project_weight,
    project_bias,
    dense_weight,
    dense_bias,
    expand_weight,
    expand_bias,
    shrink_weight,
    shrink_bias,
):
    project_full, expand_full = (
        lax.all_gather(project_weight, "fsdp", axis=0, tiled=True),
        lax.all_gather(expand_weight, "fsdp", axis=0, tiled=True),
    )
    dense_full, shrink_full = (
        lax.all_gather(dense_weight, "fsdp", axis=1, tiled=True),
        lax.all_gather(shrink_weight, "fsdp", axis=1, tiled=True),
    )
    model_width = project_full.shape[0]
    local_width = project_full.shape[2]
    heads_here = local_width // HS
    own_rows = inputs.astype(jnp.float32)
    own_grads = cotangent.astype(jnp.float32)
    first_out, first_normal, first_spread = normalize(own_rows, first_gain, first_shift)
    second_out, second_normal, second_spread = normalize(own_rows, second_gain, second_shift)
    first_normed, second_normed = (
        lax.all_gather(first_out.astype(jnp.bfloat16), "tp", axis=0, tiled=True),
        lax.all_gather(second_out.astype(jnp.bfloat16), "tp", axis=0, tiled=True),
    )
    row_count = first_normed.shape[0]
    seq_count = row_count // LEN
    block_rows = min(512, LEN)
    block_count = LEN // block_rows
    score_scale = HS ** (-0.5)
    project_flat = project_full.reshape(model_width, 3 * local_width)
    joined_rows = (
        jnp.dot(first_normed, project_flat, preferred_element_type=jnp.float32).reshape(
            row_count, 3, local_width
        )
        + project_bias[None]
    )
    cosine_table, sine_table = rotary_tables(row_count)
    queries = rotate(
        joined_rows[:, 0].reshape(row_count, heads_here, HS), cosine_table, sine_table
    ).astype(jnp.bfloat16)
    keys_all = rotate(
        joined_rows[:, 1].reshape(row_count, heads_here, HS), cosine_table, sine_table
    ).astype(jnp.bfloat16)
    values_all = joined_rows[:, 2].reshape(row_count, heads_here, HS).astype(jnp.bfloat16)

    def attend_sequence(seq_index):
        seq_start = seq_index * LEN
        seq_keys = lax.dynamic_slice_in_dim(keys_all, seq_start, LEN, 0)
        seq_values = lax.dynamic_slice_in_dim(values_all, seq_start, LEN, 0)

        def attend_block(block_index):
            first_row = block_index * block_rows
            block_queries = lax.dynamic_slice_in_dim(queries, seq_start + first_row, block_rows, 0)
            scores = causal_scores(block_queries, seq_keys, first_row, score_scale)
            row_top = jnp.max(scores, axis=-1, keepdims=True)
            shifted = jnp.exp(scores - row_top)
            row_total = jnp.sum(shifted, axis=-1, keepdims=True)
            weights_low = (shifted / row_total).astype(jnp.bfloat16)
            mixture = jnp.einsum(
                "hqk,khd->qhd", weights_low, seq_values, preferred_element_type=jnp.float32
            )
            return (mixture.astype(jnp.bfloat16), (row_top + jnp.log(row_total))[..., 0])

        return lax.map(attend_block, jnp.arange(block_count))

    context_blocks, log_totals = lax.map(attend_sequence, jnp.arange(seq_count))
    context = context_blocks.reshape(row_count, local_width)
    pre_act = jnp.dot(second_normed, expand_full, preferred_element_type=jnp.float32) + expand_bias
    activation = gelu_exact(pre_act).astype(jnp.bfloat16)
    branch = lax.psum_scatter(
        jnp.dot(context, dense_full, preferred_element_type=jnp.float32)
        + jnp.dot(activation, shrink_full, preferred_element_type=jnp.float32),
        "tp",
        scatter_dimension=0,
        tiled=True,
    )
    output = (own_rows + branch + dense_bias + shrink_bias).astype(jnp.bfloat16)
    grad_rows = lax.all_gather(cotangent, "tp", axis=0, tiled=True)
    dense_grad = jnp.dot(context.T, grad_rows, preferred_element_type=jnp.float32)
    shrink_grad = jnp.dot(activation.T, grad_rows, preferred_element_type=jnp.float32)
    context_grad = jnp.dot(grad_rows, dense_full.T, preferred_element_type=jnp.float32).astype(
        jnp.bfloat16
    )
    activation_grad = jnp.dot(grad_rows, shrink_full.T, preferred_element_type=jnp.float32)
    unused_value, gelu_pull = jax.vjp(gelu_exact, pre_act)
    pre_grad = gelu_pull(activation_grad)[0].astype(jnp.bfloat16)
    expand_grad = jnp.dot(second_normed.T, pre_grad, preferred_element_type=jnp.float32)
    expand_bias_part = jnp.sum(pre_grad.astype(jnp.float32), axis=0)
    second_grad = jnp.dot(pre_grad, expand_full.T, preferred_element_type=jnp.float32)
    context_heads = context_grad.reshape(row_count, heads_here, HS)

    def back_sequence(pack):
        seq_index, seq_totals = pack
        seq_start = seq_index * LEN
        seq_keys = lax.dynamic_slice_in_dim(keys_all, seq_start, LEN, 0)
        seq_values = lax.dynamic_slice_in_dim(values_all, seq_start, LEN, 0)

        def back_block(carry, item):
            key_sum, value_sum = carry
            block_index, block_totals = item
            first_row = block_index * block_rows
            block_queries = lax.dynamic_slice_in_dim(queries, seq_start + first_row, block_rows, 0)
            block_grads = lax.dynamic_slice_in_dim(
                context_heads, seq_start + first_row, block_rows, 0
            )
            scores = causal_scores(block_queries, seq_keys, first_row, score_scale)
            attention = jnp.exp(scores - block_totals[..., None])
            prob_grad = jnp.einsum(
                "qhd,khd->hqk", block_grads, seq_values, preferred_element_type=jnp.float32
            )
            score_grad = (
                attention * (prob_grad - jnp.sum(attention * prob_grad, axis=-1, keepdims=True))
            ).astype(jnp.bfloat16)
            query_part = (
                jnp.einsum("hqk,khd->qhd", score_grad, seq_keys, preferred_element_type=jnp.float32)
                * score_scale
            )
            key_sum = (
                key_sum
                + jnp.einsum(
                    "hqk,qhd->khd", score_grad, block_queries, preferred_element_type=jnp.float32
                )
                * score_scale
            )
            value_sum = value_sum + jnp.einsum(
                "hqk,qhd->khd",
                attention.astype(jnp.bfloat16),
                block_grads,
                preferred_element_type=jnp.float32,
            )
            return ((key_sum, value_sum), query_part)

        zero_heads = jnp.zeros((LEN, heads_here, HS), jnp.float32)
        (key_sum, value_sum), query_parts = lax.scan(
            back_block, (zero_heads, zero_heads), (jnp.arange(block_count), seq_totals)
        )
        return (query_parts.reshape(LEN, heads_here, HS), key_sum, value_sum)

    query_grad, key_grad, value_grad = lax.map(back_sequence, (jnp.arange(seq_count), log_totals))
    query_grad = rotate(query_grad.reshape(row_count, heads_here, HS), cosine_table, -sine_table)
    key_grad = rotate(key_grad.reshape(row_count, heads_here, HS), cosine_table, -sine_table)
    joined_grad = jnp.stack(
        [
            query_grad.reshape(row_count, local_width),
            key_grad.reshape(row_count, local_width),
            value_grad.reshape(row_count, local_width),
        ],
        axis=1,
    ).astype(jnp.bfloat16)
    project_bias_part = jnp.sum(joined_grad.astype(jnp.float32), axis=0)
    joined_flat = joined_grad.reshape(row_count, 3 * local_width)
    project_grad = jnp.dot(first_normed.T, joined_flat, preferred_element_type=jnp.float32).reshape(
        model_width, 3, local_width
    )
    first_grad = jnp.dot(joined_flat, project_flat.T, preferred_element_type=jnp.float32)
    first_rows, second_rows = (
        lax.psum_scatter(first_grad, "tp", scatter_dimension=0, tiled=True),
        lax.psum_scatter(second_grad, "tp", scatter_dimension=0, tiled=True),
    )
    input_grad = (
        own_grads
        + norm_back(first_rows, first_normal, first_spread, first_gain)
        + norm_back(second_rows, second_normal, second_spread, second_gain)
    )
    first_gain_part = jnp.sum(first_rows * first_normal, axis=0)
    first_shift_part = jnp.sum(first_rows, axis=0)
    second_gain_part = jnp.sum(second_rows * second_normal, axis=0)
    second_shift_part = jnp.sum(second_rows, axis=0)
    out_bias_part = jnp.sum(own_grads, axis=0)
    first_gain_grad, first_shift_grad, second_gain_grad, second_shift_grad, out_bias_grad = (
        lax.psum(
            (first_gain_part, first_shift_part, second_gain_part, second_shift_part, out_bias_part),
            ("fsdp", "tp"),
        )
    )
    project_bias_grad, expand_bias_grad = lax.psum((project_bias_part, expand_bias_part), "fsdp")
    project_weight_grad, expand_weight_grad = (
        lax.psum_scatter(project_grad, "fsdp", scatter_dimension=0, tiled=True),
        lax.psum_scatter(expand_grad, "fsdp", scatter_dimension=0, tiled=True),
    )
    dense_weight_grad, shrink_weight_grad = (
        lax.psum_scatter(dense_grad, "fsdp", scatter_dimension=1, tiled=True),
        lax.psum_scatter(shrink_grad, "fsdp", scatter_dimension=1, tiled=True),
    )
    return (
        output,
        input_grad,
        first_gain_grad,
        first_shift_grad,
        second_gain_grad,
        second_shift_grad,
        project_weight_grad,
        project_bias_grad,
        dense_weight_grad,
        out_bias_grad,
        expand_weight_grad,
        expand_bias_grad,
        shrink_weight_grad,
        out_bias_grad,
    )


def solution(mesh):
    return jax.shard_map(
        body,
        mesh=mesh,
        in_specs=(
            P(("fsdp", "tp"), None),
            P(("fsdp", "tp"), None),
            P(),
            P(),
            P(),
            P(),
            P("fsdp", None, "tp"),
            P(None, "tp"),
            P("tp", "fsdp"),
            P(),
            P("fsdp", "tp"),
            P("tp"),
            P("tp", "fsdp"),
            P(),
        ),
        out_specs=(
            P(("fsdp", "tp"), None),
            P(("fsdp", "tp"), None),
            P(),
            P(),
            P(),
            P(),
            P("fsdp", None, "tp"),
            P(None, "tp"),
            P("tp", "fsdp"),
            P(),
            P("fsdp", "tp"),
            P("tp"),
            P("tp", "fsdp"),
            P(),
        ),
        check_vma=False,
    )
```

profile of v0, /device:TPU:0, one launch (start us, length us, event | category | flops | bytes accessed | tf_op | source)
XLA Modules:
  0.0 1660.7 jit_solution(12958320723334942280)
XLA Ops:
  18.0 32.8 %all-gather.12.cloned.1.call-done = bf16[512,1024]{0,1:T(8,128)(2,1)} async-done(((bf16[512,64]{0,1:T(8,128)(2,1)}), bf16[512,1024]{0,1:T(8,128)(2,1)}) %all-gather.12.cloned.1.call-update) | async-done | bytes 1048592 | tf_op jit(solution)/shard_map/all_gather | solution.py:87
  50.8 57.3 %all-gather.20.cloned.1.call-done = bf16[2048,1024]{1,0:T(8,128)(2,1)} async-done(((bf16[1024,1024]{1,0:T(8,128)(2,1)}), bf16[2048,1024]{1,0:T(8,128)(2,1)}) %all-gather.20.cloned.1.call-update) | async-done | bytes 4194320 | tf_op jit(solution)/shard_map/all_gather | solution.py:154
  114.3 41.5 %all-gather.10.cloned.1.call-done = bf16[1024,3,512]{2,0,1:T(8,128)(2,1)} async-done(((bf16[64,3,512]{2,0,1:T(8,128)(2,1)}), bf16[1024,3,512]{2,0,1:T(8,128)(2,1)}) %all-gather.10.cloned.1.call-update) | async-done | bytes 3145744 | tf_op jit(solution)/shard_map/all_gather | solution.py:83
  160.5 51.8 %all-gather.8.cloned.1.call-done = bf16[2048,1024]{1,0:T(8,128)(2,1)} async-done(((bf16[1024,1024]{1,0:T(8,128)(2,1)}), bf16[2048,1024]{1,0:T(8,128)(2,1)}) %all-gather.8.cloned.1.call-update) | async-done | bytes 4194320 | tf_op jit(solution)/shard_map/all_gather | solution.py:98
  227.0 191.0 %while.49 = (s32[]{:T(128)}, bf16[4,512,8,64]{1,3,2,0:T(8,128)(2,1)}, f32[4,8,512]{2,1,0:T(8,128)S(1)}, s32[4]{0:T(128)S(1)}, bf16[2048,8,64]{0,2,1:T(8,128)(2,1...) while((s32[]{:T(128)}, ...), condition=%wide.region_5.6_spmd, body=%wide.region_2.5_spmd.sunk | while | flops 2249454080 | bytes 110236336 | solution.py:140
  418.0 523.5 %while.50 = (s32[]{:T(128)}, f32[2048,8,64]{0,2,1:T(8,128)}, f32[2048,8,64]{0,2,1:T(8,128)}, f32[4,512,8,64]{1,0,3,2:T(4,128)}, s32[4]{0:T(128)S(1)}, /*index=5*...) while((s32[]{:T(128)}, f32[2048,8,64]{0,2,1:T(8,128)}, ...), condition=%wide.region_9.10_spmd.clone, body=%wide.region_7.9_spmd.clone.sunk | while | flops 5450756608 | bytes 284250304 | solution.py:210
  419.4 17.4 %fusion.132 = f32[8,512,2048]{2,1,0:T(8,128)} fusion(bf16[2048,8,64]{0,2,1:T(8,128)(2,1)} %get-tuple-element.520, bf16[2048,8,64]{0,2,1:T(8,128)(2,1)} %get-tuple-element.519, s32[]{:T(128)S(6)} %select_n.101), kind=kOutput, calls=%fused_computation.28.clone.1 | convolution fusion | flops 1073741824 | bytes 36175876 | tf_op jit(solution)/shard_map/while/body/eval_jaxpr/while/body/eval_jaxpr/qhd,khd->hqk/dot_general | solution.py:184
  437.4 24.6 %multiply_reduce_fusion.4 = (f32[8,512]{1,0:T(8,128)S(1)}, f32[8,512,2048]{2,1,0:T(8,128)}) fusion(f32[8,512,2048]{2,1,0:T(8,128)} %fusion.132, f32[8,512]{1,0:T(8,128)S(1)} %dynamic-slice_bitcast_fusion.2, bf16[2048,8,64]{0,2,1:T(8,128)(2,1)S(1)} %get-tuple-element.517, bf16[2048,8,64]{0,2,1:T(8,128)(2,1)} %get-tuple-element.516, ...), kind=kOutput, calls=%fused_computation.18.clone.1 | convolution fusion | flops 1115680768 | bytes 70811648 | tf_op jit(solution)/shard_map/while/body/eval_jaxpr/while/body/eval_jaxpr/qhd,khd->hqk/dot_general | solution.py:54
  462.1 27.4 %multiply_convert_fusion.3 = bf16[8,512,2048]{2,1,0:T(8,128)(2,1)} fusion(f32[8,512,2048]{2,1,0:T(8,128)} %get-tuple-element.448, f32[8,512,2048]{2,1,0:T(8,128)} %fusion.132, f32[8,512]{1,0:T(8,128)S(1)} %get-tuple-element.449), kind=kLoop, calls=%fused_computation.17.clone.1 | loop fusion | flops 25165824 | bytes 83902464 | tf_op jit(solution)/shard_map/while/body/eval_jaxpr/while/body/eval_jaxpr/convert_element_type | solution.py:189
  499.3 21.0 %dynamic_update_slice.39 = f32[4,512,8,64]{1,0,3,2:T(4,128)} dynamic-update-slice(f32[4,512,8,64]{1,0,3,2:T(4,128)} %get-tuple-element.500, f32[1,512,8,64]{1,0,3,2:T(1,128)S(1)} %copy.59, s32[]{:T(128)} %get-tuple-element.497, s32[]{:T(128)} %constant.176.clone.1..sunk.1, s32[]{:T(128)} %constant.176.clone.1..sunk.1, s32[]{:T(128)} %constant.176.clone.1..sunk.1) | dynamic-update-slice | bytes 2097156 | tf_op jit(solution)/shard_map/while/body/eval_jaxpr/while/body/jit(dynamic_update_index_in_dim)/dynamic_update_slice | solution.py:210
  548.3 17.4 %fusion.132 = f32[8,512,2048]{2,1,0:T(8,128)} fusion(bf16[2048,8,64]{0,2,1:T(8,128)(2,1)} %get-tuple-element.520, bf16[2048,8,64]{0,2,1:T(8,128)(2,1)} %get-tuple-element.519, s32[]{:T(128)S(6)} %select_n.101), kind=kOutput, calls=%fused_computation.28.clone.1 | convolution fusion | flops 1073741824 | bytes 36175876 | tf_op jit(solution)/shard_map/while/body/eval_jaxpr/while/body/eval_jaxpr/qhd,khd->hqk/dot_general | solution.py:184
  566.4 24.6 %multiply_reduce_fusion.4 = (f32[8,512]{1,0:T(8,128)S(1)}, f32[8,512,2048]{2,1,0:T(8,128)}) fusion(f32[8,512,2048]{2,1,0:T(8,128)} %fusion.132, f32[8,512]{1,0:T(8,128)S(1)} %dynamic-slice_bitcast_fusion.2, bf16[2048,8,64]{0,2,1:T(8,128)(2,1)S(1)} %get-tuple-element.517, bf16[2048,8,64]{0,2,1:T(8,128)(2,1)} %get-tuple-element.516, ...), kind=kOutput, calls=%fused_computation.18.clone.1 | convolution fusion | flops 1115680768 | bytes 70811648 | tf_op jit(solution)/shard_map/while/body/eval_jaxpr/while/body/eval_jaxpr/qhd,khd->hqk/dot_general | solution.py:54
  591.0 27.4 %multiply_convert_fusion.3 = bf16[8,512,2048]{2,1,0:T(8,128)(2,1)} fusion(f32[8,512,2048]{2,1,0:T(8,128)} %get-tuple-element.448, f32[8,512,2048]{2,1,0:T(8,128)} %fusion.132, f32[8,512]{1,0:T(8,128)S(1)} %get-tuple-element.449), kind=kLoop, calls=%fused_computation.17.clone.1 | loop fusion | flops 25165824 | bytes 83902464 | tf_op jit(solution)/shard_map/while/body/eval_jaxpr/while/body/eval_jaxpr/convert_element_type | solution.py:189
  628.2 21.0 %dynamic_update_slice.39 = f32[4,512,8,64]{1,0,3,2:T(4,128)} dynamic-update-slice(f32[4,512,8,64]{1,0,3,2:T(4,128)} %get-tuple-element.500, f32[1,512,8,64]{1,0,3,2:T(1,128)S(1)} %copy.59, s32[]{:T(128)} %get-tuple-element.497, s32[]{:T(128)} %constant.176.clone.1..sunk.1, s32[]{:T(128)} %constant.176.clone.1..sunk.1, s32[]{:T(128)} %constant.176.clone.1..sunk.1) | dynamic-update-slice | bytes 2097156 | tf_op jit(solution)/shard_map/while/body/eval_jaxpr/while/body/jit(dynamic_update_index_in_dim)/dynamic_update_slice | solution.py:210
  661.4 17.0 %bitcast_add_fusion.5 = f32[2048,8,64]{0,2,1:T(8,128)} fusion(f32[2048,8,64]{0,2,1:T(8,128)} %get-tuple-element.499, f32[8,512,2048]{2,1,0:T(8,128)} %get-tuple-element.448, pred[]{:T(512)S(6)} %compare.4, bf16[2048,8,64]{0,2,1:T(8,128)(2,1)} %get-tuple-element.519, s32[]{:T(128)S(6)} %select_n.101), kind=kOutput, calls=%fused_computation.22.clone.1 | convolution fusion | flops 1084227584 | bytes 42467332 | tf_op jit(solution)/shard_map/while/body/eval_jaxpr/while/body/eval_jaxpr/hqk,qhd->khd/dot_general | solution.py:201
  679.7 17.4 %fusion.132 = f32[8,512,2048]{2,1,0:T(8,128)} fusion(bf16[2048,8,64]{0,2,1:T(8,128)(2,1)} %get-tuple-element.520, bf16[2048,8,64]{0,2,1:T(8,128)(2,1)} %get-tuple-element.519, s32[]{:T(128)S(6)} %select_n.101), kind=kOutput, calls=%fused_computation.28.clone.1 | convolution fusion | flops 1073741824 | bytes 36175876 | tf_op jit(solution)/shard_map/while/body/eval_jaxpr/while/body/eval_jaxpr/qhd,khd->hqk/dot_general | solution.py:184
  697.7 24.6 %multiply_reduce_fusion.4 = (f32[8,512]{1,0:T(8,128)S(1)}, f32[8,512,2048]{2,1,0:T(8,128)}) fusion(f32[8,512,2048]{2,1,0:T(8,128)} %fusion.132, f32[8,512]{1,0:T(8,128)S(1)} %dynamic-slice_bitcast_fusion.2, bf16[2048,8,64]{0,2,1:T(8,128)(2,1)S(1)} %get-tuple-element.517, bf16[2048,8,64]{0,2,1:T(8,128)(2,1)} %get-tuple-element.516, ...), kind=kOutput, calls=%fused_computation.18.clone.1 | convolution fusion | flops 1115680768 | bytes 70811648 | tf_op jit(solution)/shard_map/while/body/eval_jaxpr/while/body/eval_jaxpr/qhd,khd->hqk/dot_general | solution.py:54
  722.3 27.4 %multiply_convert_fusion.3 = bf16[8,512,2048]{2,1,0:T(8,128)(2,1)} fusion(f32[8,512,2048]{2,1,0:T(8,128)} %get-tuple-element.448, f32[8,512,2048]{2,1,0:T(8,128)} %fusion.132, f32[8,512]{1,0:T(8,128)S(1)} %get-tuple-element.449), kind=kLoop, calls=%fused_computation.17.clone.1 | loop fusion | flops 25165824 | bytes 83902464 | tf_op jit(solution)/shard_map/while/body/eval_jaxpr/while/body/eval_jaxpr/convert_element_type | solution.py:189
  759.6 21.0 %dynamic_update_slice.39 = f32[4,512,8,64]{1,0,3,2:T(4,128)} dynamic-update-slice(f32[4,512,8,64]{1,0,3,2:T(4,128)} %get-tuple-element.500, f32[1,512,8,64]{1,0,3,2:T(1,128)S(1)} %copy.59, s32[]{:T(128)} %get-tuple-element.497, s32[]{:T(128)} %constant.176.clone.1..sunk.1, s32[]{:T(128)} %constant.176.clone.1..sunk.1, s32[]{:T(128)} %constant.176.clone.1..sunk.1) | dynamic-update-slice | bytes 2097156 | tf_op jit(solution)/shard_map/while/body/eval_jaxpr/while/body/jit(dynamic_update_index_in_dim)/dynamic_update_slice | solution.py:210
  811.0 17.4 %fusion.132 = f32[8,512,2048]{2,1,0:T(8,128)} fusion(bf16[2048,8,64]{0,2,1:T(8,128)(2,1)} %get-tuple-element.520, bf16[2048,8,64]{0,2,1:T(8,128)(2,1)} %get-tuple-element.519, s32[]{:T(128)S(6)} %select_n.101), kind=kOutput, calls=%fused_computation.28.clone.1 | convolution fusion | flops 1073741824 | bytes 36175876 | tf_op jit(solution)/shard_map/while/body/eval_jaxpr/while/body/eval_jaxpr/qhd,khd->hqk/dot_general | solution.py:184
  829.0 24.6 %multiply_reduce_fusion.4 = (f32[8,512]{1,0:T(8,128)S(1)}, f32[8,512,2048]{2,1,0:T(8,128)}) fusion(f32[8,512,2048]{2,1,0:T(8,128)} %fusion.132, f32[8,512]{1,0:T(8,128)S(1)} %dynamic-slice_bitcast_fusion.2, bf16[2048,8,64]{0,2,1:T(8,128)(2,1)S(1)} %get-tuple-element.517, bf16[2048,8,64]{0,2,1:T(8,128)(2,1)} %get-tuple-element.516, ...), kind=kOutput, calls=%fused_computation.18.clone.1 | convolution fusion | flops 1115680768 | bytes 70811648 | tf_op jit(solution)/shard_map/while/body/eval_jaxpr/while/body/eval_jaxpr/qhd,khd->hqk/dot_general | solution.py:54
  853.7 27.4 %multiply_convert_fusion.3 = bf16[8,512,2048]{2,1,0:T(8,128)(2,1)} fusion(f32[8,512,2048]{2,1,0:T(8,128)} %get-tuple-element.448, f32[8,512,2048]{2,1,0:T(8,128)} %fusion.132, f32[8,512]{1,0:T(8,128)S(1)} %get-tuple-element.449), kind=kLoop, calls=%fused_computation.17.clone.1 | loop fusion | flops 25165824 | bytes 83902464 | tf_op jit(solution)/shard_map/while/body/eval_jaxpr/while/body/eval_jaxpr/convert_element_type | solution.py:189
  890.9 21.0 %dynamic_update_slice.39 = f32[4,512,8,64]{1,0,3,2:T(4,128)} dynamic-update-slice(f32[4,512,8,64]{1,0,3,2:T(4,128)} %get-tuple-element.500, f32[1,512,8,64]{1,0,3,2:T(1,128)S(1)} %copy.59, s32[]{:T(128)} %get-tuple-element.497, s32[]{:T(128)} %constant.176.clone.1..sunk.1, s32[]{:T(128)} %constant.176.clone.1..sunk.1, s32[]{:T(128)} %constant.176.clone.1..sunk.1) | dynamic-update-slice | bytes 2097156 | tf_op jit(solution)/shard_map/while/body/eval_jaxpr/while/body/jit(dynamic_update_index_in_dim)/dynamic_update_slice | solution.py:210
  981.7 49.4 %multiply_convert_fusion.1 = (bf16[2048,2048]{1,0:T(8,128)(2,1)}, f32[2048,2048]{1,0:T(8,128)}, f32[2048,2048]{1,0:T(8,128)}) fusion(f32[2048]{0:T(1024)S(1)} %copy-done.25, bf16[2048,1024]{1,0:T(8,128)(2,1)} %all-gather.14.cloned.1.call-done, bf16[1024,2048]{1,0:T(8,128)(2,1)} %all-gather.16.cloned.1.call-done), kind=kOutput, calls=%fused_computation.42 | convolution fusion | flops 8866758656 | bytes 50339840 | tf_op jit(solution)/shard_map/dot_general | solution.py:144
  1031.0 27.8 %convert_reduce_fusion = (f32[2048]{0:T(1024)S(1)}, bf16[2048,2048]{1,0:T(8,128)(2,1)}) fusion(f32[2048,2048]{1,0:T(8,128)} %get-tuple-element.306, bf16[2048,1024]{1,0:T(8,128)(2,1)} %all-gather.20.cloned.1.call-done, bf16[2048,1024]{0,1:T(8,128)(2,1)} %all-gather.18.cloned.1.call-done, f32[2048,2048]{1,0:T(8,128)} %get-tuple-element.333, ...), kind=kOutput, calls=%fused_computation.40 | convolution fusion | flops 8661235712 | bytes 50348032 | tf_op jit(solution)/shard_map/dot_general | solution.py:160
  1152.2 61.4 %all-reduce.1 = (f32[3,512]{1,0:T(4,128)}, f32[2048]{0:T(1024)}) all-reduce(f32[3,512]{1,0:T(4,128)S(1)} %copy-done.17, f32[2048]{0:T(1024)S(1)} %get-tuple-element.334), channel_id=1, replica_groups=mesh['fsdp'=16,'tp'=2] {'fsdp'}, use_global_device_ids=true, to_apply=%region_26.27 | all-reduce | flops 3584 | bytes 28672 | tf_op jit(solution)/shard_map/psum | solution.py:252
  1219.3 64.6 %reduce-scatter.8.cloned.1.call-done = f32[1024,1024]{1,0:T(8,128)} async-done(((f32[2048,1024]{1,0:T(8,128)}), f32[1024,1024]{1,0:T(8,128)}) %reduce-scatter.8.cloned.1.call-update) | async-done | bytes 4194320 | tf_op jit(solution)/shard_map/reduce_scatter | solution.py:146
  1292.4 40.1 %all-reduce = (f32[1024]{0:T(1024)}, f32[1024]{0:T(1024)}, f32[1024]{0:T(1024)}, f32[1024]{0:T(1024)}, f32[1024]{0:T(1024)S(1)}) all-reduce(f32[1024]{0:T(1024)S(1)} %get-tuple-element.252, f32[1024]{0:T(1024)S(1)} %get-tuple-element.257, f32[1024]{0:T(1024)S(1)} %get-tuple-element.261, ...), channel_id=1, replica_groups=mesh['fsdp'=16,'tp'=2] {'fsdp','tp'}, use_global_device_ids=true, to_apply=%region_17.18 | all-reduce | flops 5120 | bytes 40960 | tf_op jit(solution)/shard_map/psum | solution.py:247
  1332.5 17.6 %reduce-scatter.16.cloned.1.call-done = f32[512,64]{0,1:T(8,128)} async-done(((f32[512,1024]{0,1:T(8,128)}), f32[512,64]{0,1:T(8,128)}) %reduce-scatter.16.cloned.1.call-update) | async-done | bytes 131088 | tf_op jit(solution)/shard_map/reduce_scatter | solution.py:258
  1350.1 88.4 %reduce-scatter.14.cloned.1.call-done = f32[64,3,512]{2,0,1:T(8,128)} async-done(((f32[1024,3,512]{2,0,1:T(8,128)}), f32[64,3,512]{2,0,1:T(8,128)}) %reduce-scatter.14.cloned.1.call-update) | async-done | bytes 393232 | tf_op jit(solution)/shard_map/reduce_scatter | solution.py:254
  1438.5 107.2 %reduce-scatter.18.cloned.1.call-done = f32[64,2048]{1,0:T(8,128)} async-done(((f32[1024,2048]{1,0:T(8,128)}), f32[64,2048]{1,0:T(8,128)}) %reduce-scatter.18.cloned.1.call-update) | async-done | bytes 524304 | tf_op jit(solution)/shard_map/reduce_scatter | solution.py:255
  1545.7 107.6 %reduce-scatter.20.cloned.1.call-done = f32[2048,64]{0,1:T(8,128)} async-done(((f32[2048,1024]{0,1:T(8,128)}), f32[2048,64]{0,1:T(8,128)}) %reduce-scatter.20.cloned.1.call-update) | async-done | bytes 524304 | tf_op jit(solution)/shard_map/reduce_scatter | solution.py:259
  (196 shorter events, 513.5 us)
Async XLA Ops:
  7.2 5.0 copy-start.13
  7.2 5.0 copy-start.18
  7.2 5.0 copy-start.15
  7.2 5.0 copy-start.19
  7.2 43.6 %all-gather.12.cloned.1.call-start = ((), (), s32[]{:S(2)}) async-start(), calls=%async_computation.9 | async-start | bytes 1114112 | tf_op jit(solution)/shard_map/all_gather | solution.py:87
  8.0 100.1 %all-gather.20.cloned.1.call-start = ((), (), s32[]{:S(2)}) async-start(), calls=%async_computation.14 | async-start | bytes 6291456 | tf_op jit(solution)/shard_map/all_gather | solution.py:154
  8.7 147.1 %all-gather.10.cloned.1.call-start = ((), (), s32[]{:S(2)}) async-start(), calls=%async_computation.8 | async-start | bytes 3342336 | tf_op jit(solution)/shard_map/all_gather | solution.py:83
  9.5 202.9 %all-gather.8.cloned.1.call-start = ((), (), s32[]{:S(2)}) async-start(), calls=%async_computation.7 | async-start | bytes 6291456 | tf_op jit(solution)/shard_map/all_gather | solution.py:98
  15.0 966.0 %all-gather.14.cloned.1.call-start = ((), (), s32[]{:S(2)}) async-start(), calls=%async_computation.10 | async-start | bytes 6291456 | tf_op jit(solution)/shard_map/all_gather | solution.py:99
  15.6 965.5 %all-gather.16.cloned.1.call-start = ((), (), s32[]{:S(2)}) async-start(), calls=%async_computation.11 | async-start | bytes 4456448 | tf_op jit(solution)/shard_map/all_gather | solution.py:84
  16.2 1014.8 %all-gather.18.cloned.1.call-start = ((), (), s32[]{:S(2)}) async-start(), calls=%async_computation.12 | async-start | bytes 4456448 | tf_op jit(solution)/shard_map/all_gather | solution.py:88
  17.0 1196.7 %reduce-scatter.10.cloned.1.call-start = ((), (), s32[]{:S(2)}) async-start(), calls=%async_computation.15 | async-start | bytes 12582912 | tf_op jit(solution)/shard_map/reduce_scatter | solution.py:233
  18.0 207.1 %copy-start.6 = (f32[2048,8]{0,1:T(8,128)}, f32[2048,8]{0,1:T(8,128)S(1)}, u32[]{:S(2)}) copy-start(f32[2048,8]{0,1:T(8,128)S(1)} %get-tuple-element.332) | copy-start | bytes 196612
  114.3 98.0 %copy-start.24 = (f32[3,512]{1,0:T(4,128)S(1)}, f32[3,512]{1,0:T(4,128)}, u32[]{:S(2)}) copy-start(f32[3,512]{1,0:T(4,128)} %param.25) | copy-start | bytes 18436
  947.5 5.4 copy-start.7
  947.5 5.4 copy-start.8
  964.9 7.1 copy-start.3
  981.0 232.6 %reduce-scatter.12.cloned.1.call-start = ((), (), s32[]{:S(2)}) async-start(), calls=%async_computation.16 | async-start | bytes 12582912 | tf_op jit(solution)/shard_map/reduce_scatter | solution.py:234
  1073.4 210.5 %reduce-scatter.8.cloned.1.call-start = ((), (), s32[]{:S(2)}) async-start(), calls=%async_computation.13 | async-start | bytes 12582912 | tf_op jit(solution)/shard_map/reduce_scatter | solution.py:146
  1077.2 11.4 copy-start.5
  1094.3 255.8 %reduce-scatter.16.cloned.1.call-start = ((), (), s32[]{:S(2)}) async-start(), calls=%async_computation.18 | async-start | bytes 2228224 | tf_op jit(solution)/shard_map/reduce_scatter | solution.py:258
  1100.3 338.2 %reduce-scatter.14.cloned.1.call-start = ((), (), s32[]{:S(2)}) async-start(), calls=%async_computation.17 | async-start | bytes 6684672 | tf_op jit(solution)/shard_map/reduce_scatter | solution.py:254
  1121.5 424.2 %reduce-scatter.18.cloned.1.call-start = ((), (), s32[]{:S(2)}) async-start(), calls=%async_computation.19 | async-start | bytes 8912896 | tf_op jit(solution)/shard_map/reduce_scatter | solution.py:255
  1136.4 517.0 %reduce-scatter.20.cloned.1.call-start = ((), (), s32[]{:S(2)}) async-start(), calls=%async_computation.20 | async-start | bytes 8912896 | tf_op jit(solution)/shard_map/reduce_scatter | solution.py:259
  1151.5 62.1 %copy-start.1 = (bf16[1024,1024]{1,0:T(8,128)(2,1)S(1)}, bf16[1024,1024]{1,0:T(8,128)(2,1)}, u32[]{:S(2)}) copy-start(bf16[1024,1024]{1,0:T(8,128)(2,1)} %param.18) | copy-start | bytes 6291460
  1151.5 62.1 %copy-start.10 = (f32[1024]{0:T(1024)S(1)}, f32[1024]{0:T(1024)}, u32[]{:S(2)}) copy-start(f32[1024]{0:T(1024)} %copy-done.9) | copy-start | bytes 12292
  1151.5 62.1 %copy-start.12 = (f32[1024]{0:T(1024)S(1)}, f32[1024]{0:T(1024)}, u32[]{:S(2)}) copy-start(f32[1024]{0:T(1024)} %copy-done.11) | copy-start | bytes 12292
  1151.5 62.1 %copy-start.14 = (f32[1024]{0:T(1024)S(1)}, f32[1024]{0:T(1024)}, u32[]{:S(2)}) copy-start(f32[1024]{0:T(1024)} %param.20) | copy-start | bytes 12292
  1151.5 62.1 %copy-start.16 = (f32[1024]{0:T(1024)S(1)}, f32[1024]{0:T(1024)}, u32[]{:S(2)}) copy-start(f32[1024]{0:T(1024)} %param.22) | copy-start | bytes 12292
  1213.6 70.3 %copy-start.20 = (f32[1024]{0:T(1024)S(1)}, f32[1024]{0:T(1024)}, u32[]{:S(2)}) copy-start(f32[1024]{0:T(1024)} %param.31) | copy-start | bytes 12292
  1213.6 70.3 %copy-start.21 = (f32[1024]{0:T(1024)S(1)}, f32[1024]{0:T(1024)}, u32[]{:S(2)}) copy-start(f32[1024]{0:T(1024)} %param.27) | copy-start | bytes 12292
  1332.5 321.4 %copy-start.22 = (f32[1024]{0:T(1024)}, f32[1024]{0:T(1024)S(1)}, u32[]{:S(2)}) copy-start(f32[1024]{0:T(1024)S(1)} %get-tuple-element.552) | copy-start | bytes 12292
  (8 other events, 18.6 us)
Sparse Core Ops, SparseCore 0:
  10.2 40.5 all-gather.11
  52.3 55.6 all-gather.19
  110.3 45.4 all-gather.9
  157.2 55.0 all-gather.7
  213.7 56.7 all-gather.13
  272.5 50.4 all-gather.15
  325.1 48.8 all-gather.17
  981.1 99.5 reduce-scatter.9
  1083.0 99.3 reduce-scatter.11
  1184.5 99.3 reduce-scatter.7
  1288.2 61.8 reduce-scatter.15
  1354.4 83.9 reduce-scatter.13
  1443.1 102.5 reduce-scatter.17
  1550.2 103.0 reduce-scatter.19
where the time goes:
time: 1670 us; the launch traced here: 1660 us
  matrix products  621 us (37%)
  waiting for transfers between devices  573 us (34%)
  other arithmetic  206 us (12%)
  local copies, waits for them, and re-layouts  138 us (8%)
  blocking collectives  101 us (6%)
    dot_general x8, matrix products, causal_scores(): jnp.einsum('qhd,khd->hqk', query_rows, key_rows, preferred_element_type=j...  158 us
    convert_element_type x4, other arithmetic, back_block(): score_grad = (attention * (prob_grad - jnp.sum(attention * prob_grad, axi...  110 us
    reduce_scatter x1, waiting for transfers between devices, body(): lax.psum_scatter(shrink_grad, 'fsdp', scatter_dimension=1, tiled=True)  108 us
    reduce_scatter x1, waiting for transfers between devices, body(): lax.psum_scatter(expand_grad, 'fsdp', scatter_dimension=0, tiled=True)  107 us
    reduce_scatter x1, waiting for transfers between devices, body(): lax.psum_scatter(project_grad, 'fsdp', scatter_dimension=0, tiled=True)  88.4 us
    dynamic_update_slice x8, local copies, waits for them, and re-layouts, back_sequence(): lax.scan(back_block, (zero_heads, zero_heads), (jnp.arange(block_count),...  88.3 us
    dot_general x4, matrix products, back_block(): jnp.einsum('qhd,khd->hqk', block_grads, seq_values, preferred_element_typ...  69.5 us
    dot_general x4, matrix products, back_block(): jnp.einsum('hqk,qhd->khd', attention.astype(jnp.bfloat16), block_grads, p...  66.8 us
  transfers between devices with their start and end apart: 14, of which 9 were waited for; matrix products, arithmetic and copies ran while one was open for 58% of the time, Pallas kernels for 0%

commit v1 on v0

--- a/solution.py
+++ b/solution.py
@@ -7,6 +7,15 @@
 ROT = 16
 LEN = 2048
 EPS = 1e-05
+
+
+def region_create(matrix):
+    log = []
+    for _ in range(lax.axis_size("fsdp")):
+        log.append(matrix)
+    return jnp.concatenate(
+        lax.all_to_all(jnp.stack(log, axis=0), axis_name="fsdp", concat_axis=0, split_axis=0), 0
+    )
 
 
 def normalize(values, gain_vector, shift_vector):
@@ -80,7 +89,7 @@
     shrink_bias,
 ):
     project_full, expand_full = (
-        lax.all_gather(project_weight, "fsdp", axis=0, tiled=True),
+        region_create(project_weight),
         lax.all_gather(expand_weight, "fsdp", axis=0, tiled=True),
     )
     dense_full, shrink_full = (

time: 1670 us -> 1650 us (0.988)
  waiting for transfers between devices: 573 us -> 556 us
    all_gather x1 -> x0, waiting for transfers between devices: 41.5 us -> none  [body(): lax.all_gather(project_weight, 'fsdp', axis=0, tiled=True)]
    all_gather x1, waiting for transfers between devices: 32.8 us -> 52.8 us  [body(): lax.all_gather(dense_weight, 'fsdp', axis=1, tiled=True)]
  transfers between devices with their start and end apart: 14 -> 14, of which waited for: 9 -> 8; matrix products, arithmetic and copies ran while one was open for 58% -> 58% of each run, Pallas kernels for 0% -> 0%
where the time goes in v1:
time: 1650 us; the launch traced here: 1640 us
  matrix products  624 us (38%)
  waiting for transfers between devices  556 us (34%)
  other arithmetic  202 us (12%)
  local copies, waits for them, and re-layouts  131 us (8%)
  blocking collectives  101 us (6%)
    dot_general x8, matrix products, causal_scores(): jnp.einsum('qhd,khd->hqk', query_rows, key_rows, preferred_element_type=j...  159 us
    convert_element_type x4, other arithmetic, back_block(): score_grad = (attention * (prob_grad - jnp.sum(attention * prob_grad, axi...  110 us
    reduce_scatter x1, waiting for transfers between devices, body(): lax.psum_scatter(shrink_grad, 'fsdp', scatter_dimension=1, tiled=True)  108 us
    reduce_scatter x1, waiting for transfers between devices, body(): lax.psum_scatter(expand_grad, 'fsdp', scatter_dimension=0, tiled=True)  107 us
    reduce_scatter x1, waiting for transfers between devices, body(): lax.psum_scatter(project_grad, 'fsdp', scatter_dimension=0, tiled=True)  88.6 us
    dynamic_update_slice x8, local copies, waits for them, and re-layouts, back_sequence(): lax.scan(back_block, (zero_heads, zero_heads), (jnp.arange(block_count),...  88.4 us
    reduce_scatter x1, waiting for transfers between devices, body(): lax.psum_scatter(jnp.dot(context, dense_full, preferred_element_type=jnp....  73.4 us
    dot_general x4, matrix products, back_block(): jnp.einsum('qhd,khd->hqk', block_grads, seq_values, preferred_element_typ...  69.5 us
  transfers between devices with their start and end apart: 14, of which 8 were waited for; matrix products, arithmetic and copies ran while one was open for 58% of the time, Pallas kernels for 0%

profile of v1, /device:TPU:0, one launch (start us, length us, event | category | flops | bytes accessed | tf_op | source)
XLA Modules:
  0.0 1644.6 jit_solution(14907341609069775003)
XLA Ops:
  26.8 52.8 %all-gather.9.cloned.1.call-done = bf16[512,1024]{0,1:T(8,128)(2,1)} async-done(((bf16[512,64]{0,1:T(8,128)(2,1)}), bf16[512,1024]{0,1:T(8,128)(2,1)}) %all-gather.9.cloned.1.call-update) | async-done | bytes 1048592 | tf_op jit(solution)/shard_map/all_gather | solution.py:96
  79.6 60.4 %all-gather.17.cloned.1.call-done = bf16[2048,1024]{1,0:T(8,128)(2,1)} async-done(((bf16[1024,1024]{1,0:T(8,128)(2,1)}), bf16[2048,1024]{1,0:T(8,128)(2,1)}) %all-gather.17.cloned.1.call-update) | async-done | bytes 4194320 | tf_op jit(solution)/shard_map/all_gather | solution.py:163
  153.4 44.9 %all-gather.7.cloned.1.call-done = bf16[2048,1024]{1,0:T(8,128)(2,1)} async-done(((bf16[1024,1024]{1,0:T(8,128)(2,1)}), bf16[2048,1024]{1,0:T(8,128)(2,1)}) %all-gather.7.cloned.1.call-update) | async-done | bytes 4194320 | tf_op jit(solution)/shard_map/all_gather | solution.py:107
  221.3 191.5 %while.49 = (s32[]{:T(128)}, bf16[4,512,8,64]{1,3,2,0:T(8,128)(2,1)}, f32[4,8,512]{2,1,0:T(8,128)S(1)}, s32[4]{0:T(128)S(1)}, bf16[2048,8,64]{0,2,1:T(8,128)(2,1...) while((s32[]{:T(128)}, ...), condition=%wide.region_5.6_spmd, body=%wide.region_2.5_spmd.sunk | while | flops 2249454080 | bytes 110236336 | solution.py:149
  412.8 524.1 %while.50 = (s32[]{:T(128)}, f32[2048,8,64]{0,2,1:T(8,128)}, f32[2048,8,64]{0,2,1:T(8,128)}, f32[4,512,8,64]{1,0,3,2:T(4,128)}, s32[4]{0:T(128)S(1)}, /*index=5*...) while((s32[]{:T(128)}, f32[2048,8,64]{0,2,1:T(8,128)}, ...), condition=%wide.region_9.10_spmd.clone, body=%wide.region_7.9_spmd.clone.sunk | while | flops 5450756608 | bytes 284250304 | solution.py:219
  414.2 17.4 %fusion.133 = f32[8,512,2048]{2,1,0:T(8,128)} fusion(bf16[2048,8,64]{0,2,1:T(8,128)(2,1)} %get-tuple-element.520, bf16[2048,8,64]{0,2,1:T(8,128)(2,1)} %get-tuple-element.519, s32[]{:T(128)S(6)} %select_n.101), kind=kOutput, calls=%fused_computation.28.clone.1 | convolution fusion | flops 1073741824 | bytes 36175876 | tf_op jit(solution)/shard_map/while/body/eval_jaxpr/while/body/eval_jaxpr/qhd,khd->hqk/dot_general | solution.py:193
  432.3 24.7 %multiply_reduce_fusion.4 = (f32[8,512]{1,0:T(8,128)S(1)}, f32[8,512,2048]{2,1,0:T(8,128)}) fusion(f32[8,512,2048]{2,1,0:T(8,128)} %fusion.133, f32[8,512]{1,0:T(8,128)S(1)} %dynamic-slice_bitcast_fusion.2, bf16[2048,8,64]{0,2,1:T(8,128)(2,1)S(1)} %get-tuple-element.517, bf16[2048,8,64]{0,2,1:T(8,128)(2,1)} %get-tuple-element.516, ...), kind=kOutput, calls=%fused_computation.18.clone.1 | convolution fusion | flops 1115680768 | bytes 70811648 | tf_op jit(solution)/shard_map/while/body/eval_jaxpr/while/body/eval_jaxpr/qhd,khd->hqk/dot_general | solution.py:63
  457.0 27.4 %multiply_convert_fusion.3 = bf16[8,512,2048]{2,1,0:T(8,128)(2,1)} fusion(f32[8,512,2048]{2,1,0:T(8,128)} %get-tuple-element.448, f32[8,512,2048]{2,1,0:T(8,128)} %fusion.133, f32[8,512]{1,0:T(8,128)S(1)} %get-tuple-element.449), kind=kLoop, calls=%fused_computation.17.clone.1 | loop fusion | flops 25165824 | bytes 83902464 | tf_op jit(solution)/shard_map/while/body/eval_jaxpr/while/body/eval_jaxpr/convert_element_type | solution.py:198
  494.2 21.0 %dynamic_update_slice.39 = f32[4,512,8,64]{1,0,3,2:T(4,128)} dynamic-update-slice(f32[4,512,8,64]{1,0,3,2:T(4,128)} %get-tuple-element.500, f32[1,512,8,64]{1,0,3,2:T(1,128)S(1)} %copy.60, s32[]{:T(128)} %get-tuple-element.497, s32[]{:T(128)} %constant.176.clone.1..sunk.1, s32[]{:T(128)} %constant.176.clone.1..sunk.1, s32[]{:T(128)} %constant.176.clone.1..sunk.1) | dynamic-update-slice | bytes 2097156 | tf_op jit(solution)/shard_map/while/body/eval_jaxpr/while/body/jit(dynamic_update_index_in_dim)/dynamic_update_slice | solution.py:219
  543.3 17.4 %fusion.133 = f32[8,512,2048]{2,1,0:T(8,128)} fusion(bf16[2048,8,64]{0,2,1:T(8,128)(2,1)} %get-tuple-element.520, bf16[2048,8,64]{0,2,1:T(8,128)(2,1)} %get-tuple-element.519, s32[]{:T(128)S(6)} %select_n.101), kind=kOutput, calls=%fused_computation.28.clone.1 | convolution fusion | flops 1073741824 | bytes 36175876 | tf_op jit(solution)/shard_map/while/body/eval_jaxpr/while/body/eval_jaxpr/qhd,khd->hqk/dot_general | solution.py:193
  561.4 24.7 %multiply_reduce_fusion.4 = (f32[8,512]{1,0:T(8,128)S(1)}, f32[8,512,2048]{2,1,0:T(8,128)}) fusion(f32[8,512,2048]{2,1,0:T(8,128)} %fusion.133, f32[8,512]{1,0:T(8,128)S(1)} %dynamic-slice_bitcast_fusion.2, bf16[2048,8,64]{0,2,1:T(8,128)(2,1)S(1)} %get-tuple-element.517, bf16[2048,8,64]{0,2,1:T(8,128)(2,1)} %get-tuple-element.516, ...), kind=kOutput, calls=%fused_computation.18.clone.1 | convolution fusion | flops 1115680768 | bytes 70811648 | tf_op jit(solution)/shard_map/while/body/eval_jaxpr/while/body/eval_jaxpr/qhd,khd->hqk/dot_general | solution.py:63
  586.1 27.4 %multiply_convert_fusion.3 = bf16[8,512,2048]{2,1,0:T(8,128)(2,1)} fusion(f32[8,512,2048]{2,1,0:T(8,128)} %get-tuple-element.448, f32[8,512,2048]{2,1,0:T(8,128)} %fusion.133, f32[8,512]{1,0:T(8,128)S(1)} %get-tuple-element.449), kind=kLoop, calls=%fused_computation.17.clone.1 | loop fusion | flops 25165824 | bytes 83902464 | tf_op jit(solution)/shard_map/while/body/eval_jaxpr/while/body/eval_jaxpr/convert_element_type | solution.py:198
  623.3 21.0 %dynamic_update_slice.39 = f32[4,512,8,64]{1,0,3,2:T(4,128)} dynamic-update-slice(f32[4,512,8,64]{1,0,3,2:T(4,128)} %get-tuple-element.500, f32[1,512,8,64]{1,0,3,2:T(1,128)S(1)} %copy.60, s32[]{:T(128)} %get-tuple-element.497, s32[]{:T(128)} %constant.176.clone.1..sunk.1, s32[]{:T(128)} %constant.176.clone.1..sunk.1, s32[]{:T(128)} %constant.176.clone.1..sunk.1) | dynamic-update-slice | bytes 2097156 | tf_op jit(solution)/shard_map/while/body/eval_jaxpr/while/body/jit(dynamic_update_index_in_dim)/dynamic_update_slice | solution.py:219
  656.6 17.0 %bitcast_add_fusion.5 = f32[2048,8,64]{0,2,1:T(8,128)} fusion(f32[2048,8,64]{0,2,1:T(8,128)} %get-tuple-element.499, f32[8,512,2048]{2,1,0:T(8,128)} %get-tuple-element.448, pred[]{:T(512)S(6)} %compare.4, bf16[2048,8,64]{0,2,1:T(8,128)(2,1)} %get-tuple-element.519, s32[]{:T(128)S(6)} %select_n.101), kind=kOutput, calls=%fused_computation.22.clone.1 | convolution fusion | flops 1084227584 | bytes 42467332 | tf_op jit(solution)/shard_map/while/body/eval_jaxpr/while/body/eval_jaxpr/hqk,qhd->khd/dot_general | solution.py:210
  674.8 17.4 %fusion.133 = f32[8,512,2048]{2,1,0:T(8,128)} fusion(bf16[2048,8,64]{0,2,1:T(8,128)(2,1)} %get-tuple-element.520, bf16[2048,8,64]{0,2,1:T(8,128)(2,1)} %get-tuple-element.519, s32[]{:T(128)S(6)} %select_n.101), kind=kOutput, calls=%fused_computation.28.clone.1 | convolution fusion | flops 1073741824 | bytes 36175876 | tf_op jit(solution)/shard_map/while/body/eval_jaxpr/while/body/eval_jaxpr/qhd,khd->hqk/dot_general | solution.py:193
  692.9 24.7 %multiply_reduce_fusion.4 = (f32[8,512]{1,0:T(8,128)S(1)}, f32[8,512,2048]{2,1,0:T(8,128)}) fusion(f32[8,512,2048]{2,1,0:T(8,128)} %fusion.133, f32[8,512]{1,0:T(8,128)S(1)} %dynamic-slice_bitcast_fusion.2, bf16[2048,8,64]{0,2,1:T(8,128)(2,1)S(1)} %get-tuple-element.517, bf16[2048,8,64]{0,2,1:T(8,128)(2,1)} %get-tuple-element.516, ...), kind=kOutput, calls=%fused_computation.18.clone.1 | convolution fusion | flops 1115680768 | bytes 70811648 | tf_op jit(solution)/shard_map/while/body/eval_jaxpr/while/body/eval_jaxpr/qhd,khd->hqk/dot_general | solution.py:63
  717.6 27.4 %multiply_convert_fusion.3 = bf16[8,512,2048]{2,1,0:T(8,128)(2,1)} fusion(f32[8,512,2048]{2,1,0:T(8,128)} %get-tuple-element.448, f32[8,512,2048]{2,1,0:T(8,128)} %fusion.133, f32[8,512]{1,0:T(8,128)S(1)} %get-tuple-element.449), kind=kLoop, calls=%fused_computation.17.clone.1 | loop fusion | flops 25165824 | bytes 83902464 | tf_op jit(solution)/shard_map/while/body/eval_jaxpr/while/body/eval_jaxpr/convert_element_type | solution.py:198
  754.8 21.0 %dynamic_update_slice.39 = f32[4,512,8,64]{1,0,3,2:T(4,128)} dynamic-update-slice(f32[4,512,8,64]{1,0,3,2:T(4,128)} %get-tuple-element.500, f32[1,512,8,64]{1,0,3,2:T(1,128)S(1)} %copy.60, s32[]{:T(128)} %get-tuple-element.497, s32[]{:T(128)} %constant.176.clone.1..sunk.1, s32[]{:T(128)} %constant.176.clone.1..sunk.1, s32[]{:T(128)} %constant.176.clone.1..sunk.1) | dynamic-update-slice | bytes 2097156 | tf_op jit(solution)/shard_map/while/body/eval_jaxpr/while/body/jit(dynamic_update_index_in_dim)/dynamic_update_slice | solution.py:219
  806.3 17.4 %fusion.133 = f32[8,512,2048]{2,1,0:T(8,128)} fusion(bf16[2048,8,64]{0,2,1:T(8,128)(2,1)} %get-tuple-element.520, bf16[2048,8,64]{0,2,1:T(8,128)(2,1)} %get-tuple-element.519, s32[]{:T(128)S(6)} %select_n.101), kind=kOutput, calls=%fused_computation.28.clone.1 | convolution fusion | flops 1073741824 | bytes 36175876 | tf_op jit(solution)/shard_map/while/body/eval_jaxpr/while/body/eval_jaxpr/qhd,khd->hqk/dot_general | solution.py:193
  824.3 24.7 %multiply_reduce_fusion.4 = (f32[8,512]{1,0:T(8,128)S(1)}, f32[8,512,2048]{2,1,0:T(8,128)}) fusion(f32[8,512,2048]{2,1,0:T(8,128)} %fusion.133, f32[8,512]{1,0:T(8,128)S(1)} %dynamic-slice_bitcast_fusion.2, bf16[2048,8,64]{0,2,1:T(8,128)(2,1)S(1)} %get-tuple-element.517, bf16[2048,8,64]{0,2,1:T(8,128)(2,1)} %get-tuple-element.516, ...), kind=kOutput, calls=%fused_computation.18.clone.1 | convolution fusion | flops 1115680768 | bytes 70811648 | tf_op jit(solution)/shard_map/while/body/eval_jaxpr/while/body/eval_jaxpr/qhd,khd->hqk/dot_general | solution.py:63
  849.1 27.4 %multiply_convert_fusion.3 = bf16[8,512,2048]{2,1,0:T(8,128)(2,1)} fusion(f32[8,512,2048]{2,1,0:T(8,128)} %get-tuple-element.448, f32[8,512,2048]{2,1,0:T(8,128)} %fusion.133, f32[8,512]{1,0:T(8,128)S(1)} %get-tuple-element.449), kind=kLoop, calls=%fused_computation.17.clone.1 | loop fusion | flops 25165824 | bytes 83902464 | tf_op jit(solution)/shard_map/while/body/eval_jaxpr/while/body/eval_jaxpr/convert_element_type | solution.py:198
  886.3 21.0 %dynamic_update_slice.39 = f32[4,512,8,64]{1,0,3,2:T(4,128)} dynamic-update-slice(f32[4,512,8,64]{1,0,3,2:T(4,128)} %get-tuple-element.500, f32[1,512,8,64]{1,0,3,2:T(1,128)S(1)} %copy.60, s32[]{:T(128)} %get-tuple-element.497, s32[]{:T(128)} %constant.176.clone.1..sunk.1, s32[]{:T(128)} %constant.176.clone.1..sunk.1, s32[]{:T(128)} %constant.176.clone.1..sunk.1) | dynamic-update-slice | bytes 2097156 | tf_op jit(solution)/shard_map/while/body/eval_jaxpr/while/body/jit(dynamic_update_index_in_dim)/dynamic_update_slice | solution.py:219
  919.5 17.0 %bitcast_add_fusion.5 = f32[2048,8,64]{0,2,1:T(8,128)} fusion(f32[2048,8,64]{0,2,1:T(8,128)} %get-tuple-element.499, f32[8,512,2048]{2,1,0:T(8,128)} %get-tuple-element.448, pred[]{:T(512)S(6)} %compare.4, bf16[2048,8,64]{0,2,1:T(8,128)(2,1)} %get-tuple-element.519, s32[]{:T(128)S(6)} %select_n.101), kind=kOutput, calls=%fused_computation.22.clone.1 | convolution fusion | flops 1084227584 | bytes 42467332 | tf_op jit(solution)/shard_map/while/body/eval_jaxpr/while/body/eval_jaxpr/hqk,qhd->khd/dot_general | solution.py:210
  965.7 49.3 %multiply_convert_fusion.1 = (bf16[2048,2048]{1,0:T(8,128)(2,1)}, f32[2048,2048]{1,0:T(8,128)}, f32[2048,2048]{1,0:T(8,128)}) fusion(f32[2048]{0:T(1024)S(1)} %copy-done.28, bf16[2048,1024]{1,0:T(8,128)(2,1)} %all-gather.11.cloned.1.call-done, bf16[1024,2048]{1,0:T(8,128)(2,1)} %all-gather.13.cloned.1.call-done), kind=kOutput, calls=%fused_computation.42 | convolution fusion | flops 8866758656 | bytes 50339840 | tf_op jit(solution)/shard_map/dot_general | solution.py:153
  1015.0 27.8 %convert_reduce_fusion = (f32[2048]{0:T(1024)S(1)}, bf16[2048,2048]{1,0:T(8,128)(2,1)}) fusion(f32[2048,2048]{1,0:T(8,128)} %get-tuple-element.306, bf16[2048,1024]{1,0:T(8,128)(2,1)} %all-gather.17.cloned.1.call-done, bf16[2048,1024]{0,1:T(8,128)(2,1)} %all-gather.15.cloned.1.call-done, f32[2048,2048]{1,0:T(8,128)} %get-tuple-element.333, ...), kind=kOutput, calls=%fused_computation.40 | convolution fusion | flops 8661235712 | bytes 50348032 | tf_op jit(solution)/shard_map/dot_general | solution.py:169
  1127.3 61.1 %all-reduce.1 = (f32[3,512]{1,0:T(4,128)}, f32[2048]{0:T(1024)}) all-reduce(f32[3,512]{1,0:T(4,128)S(1)} %copy-done.20, f32[2048]{0:T(1024)S(1)} %get-tuple-element.334), channel_id=1, replica_groups=mesh['fsdp'=16,'tp'=2] {'fsdp'}, use_global_device_ids=true, to_apply=%region_26.27 | all-reduce | flops 3584 | bytes 28672 | tf_op jit(solution)/shard_map/psum | solution.py:261
  1194.4 73.4 %reduce-scatter.8.cloned.1.call-done = f32[1024,1024]{1,0:T(8,128)} async-done(((f32[2048,1024]{1,0:T(8,128)}), f32[1024,1024]{1,0:T(8,128)}) %reduce-scatter.8.cloned.1.call-update) | async-done | bytes 4194320 | tf_op jit(solution)/shard_map/reduce_scatter | solution.py:155
  1276.4 39.9 %all-reduce = (f32[1024]{0:T(1024)}, f32[1024]{0:T(1024)}, f32[1024]{0:T(1024)}, f32[1024]{0:T(1024)}, f32[1024]{0:T(1024)S(1)}) all-reduce(f32[1024]{0:T(1024)S(1)} %get-tuple-element.252, f32[1024]{0:T(1024)S(1)} %get-tuple-element.257, f32[1024]{0:T(1024)S(1)} %get-tuple-element.261, ...), channel_id=1, replica_groups=mesh['fsdp'=16,'tp'=2] {'fsdp','tp'}, use_global_device_ids=true, to_apply=%region_17.18 | all-reduce | flops 5120 | bytes 40960 | tf_op jit(solution)/shard_map/psum | solution.py:256
  1316.3 17.6 %reduce-scatter.16.cloned.1.call-done = f32[512,64]{0,1:T(8,128)} async-done(((f32[512,1024]{0,1:T(8,128)}), f32[512,64]{0,1:T(8,128)}) %reduce-scatter.16.cloned.1.call-update) | async-done | bytes 131088 | tf_op jit(solution)/shard_map/reduce_scatter | solution.py:267
  1333.9 88.6 %reduce-scatter.14.cloned.1.call-done = f32[64,3,512]{2,0,1:T(8,128)} async-done(((f32[1024,3,512]{2,0,1:T(8,128)}), f32[64,3,512]{2,0,1:T(8,128)}) %reduce-scatter.14.cloned.1.call-update) | async-done | bytes 393232 | tf_op jit(solution)/shard_map/reduce_scatter | solution.py:263
  1422.4 107.2 %reduce-scatter.18.cloned.1.call-done = f32[64,2048]{1,0:T(8,128)} async-done(((f32[1024,2048]{1,0:T(8,128)}), f32[64,2048]{1,0:T(8,128)}) %reduce-scatter.18.cloned.1.call-update) | async-done | bytes 524304 | tf_op jit(solution)/shard_map/reduce_scatter | solution.py:264
  1529.6 107.7 %reduce-scatter.20.cloned.1.call-done = f32[2048,64]{0,1:T(8,128)} async-done(((f32[2048,1024]{0,1:T(8,128)}), f32[2048,64]{0,1:T(8,128)}) %reduce-scatter.20.cloned.1.call-update) | async-done | bytes 524304 | tf_op jit(solution)/shard_map/reduce_scatter | solution.py:268
  (200 shorter events, 496.6 us)
Async XLA Ops:
  7.2 4.2 copy-start.16
  7.2 4.2 copy-start.21
  7.2 4.2 copy-start.18
  7.2 72.4 %all-gather.9.cloned.1.call-start = ((), (), s32[]{:S(2)}) async-start(), calls=%async_computation.9 | async-start | bytes 1114112 | tf_op jit(solution)/shard_map/all_gather | solution.py:96
  8.0 132.1 %all-gather.17.cloned.1.call-start = ((), (), s32[]{:S(2)}) async-start(), calls=%async_computation.14 | async-start | bytes 6291456 | tf_op jit(solution)/shard_map/all_gather | solution.py:163
  8.7 189.6 %all-gather.7.cloned.1.call-start = ((), (), s32[]{:S(2)}) async-start(), calls=%async_computation.8 | async-start | bytes 6291456 | tf_op jit(solution)/shard_map/all_gather | solution.py:107
  14.3 950.8 %all-gather.11.cloned.1.call-start = ((), (), s32[]{:S(2)}) async-start(), calls=%async_computation.10 | async-start | bytes 6291456 | tf_op jit(solution)/shard_map/all_gather | solution.py:108
  14.9 950.3 %all-gather.13.cloned.1.call-start = ((), (), s32[]{:S(2)}) async-start(), calls=%async_computation.11 | async-start | bytes 4456448 | tf_op jit(solution)/shard_map/all_gather | solution.py:93
  17.5 128.7 %all-to-all-start = ((bf16[16,64,3,512]{3,1,2,0:T(8,128)(2,1)}), bf16[16,64,3,512]{3,1,2,0:T(8,128)(2,1)S(1)}, u32[]{:S(2)}, u32[]{:S(2)}) async-start(bf16[16,64,3,512]{3,1,2,0:T(8,128)(2,1)} %stack.4), calls=%async_computation | async-start | bytes 6291456 | tf_op jit(solution)/shard_map/all_to_all | solution.py:17
  24.9 990.1 %all-gather.15.cloned.1.call-start = ((), (), s32[]{:S(2)}) async-start(), calls=%async_computation.12 | async-start | bytes 4456448 | tf_op jit(solution)/shard_map/all_gather | solution.py:97
  25.5 1163.0 %reduce-scatter.10.cloned.1.call-start = ((), (), s32[]{:S(2)}) async-start(), calls=%async_computation.15 | async-start | bytes 12582912 | tf_op jit(solution)/shard_map/reduce_scatter | solution.py:242
  26.8 192.6 %copy-start.8 = (f32[2048,8]{0,1:T(8,128)}, f32[2048,8]{0,1:T(8,128)S(1)}, u32[]{:S(2)}) copy-start(f32[2048,8]{0,1:T(8,128)S(1)} %get-tuple-element.332) | copy-start | bytes 196612
  150.0 60.6 %copy-start.3 = (bf16[128,8,3,512]{3,1,2,0:T(8,128)(2,1)}, bf16[128,8,3,512]{3,1,2,0:T(8,128)(2,1)S(1)}, u32[]{:S(2)}) copy-start(bf16[128,8,3,512]{3,1,2,0:T(8,128)(2,1)S(1)} %copy.57) | copy-start | bytes 9437188
  150.0 48.3 %copy-start.27 = (f32[3,512]{1,0:T(4,128)S(1)}, f32[3,512]{1,0:T(4,128)}, u32[]{:S(2)}) copy-start(f32[3,512]{1,0:T(4,128)} %param.25) | copy-start | bytes 18436
  943.0 4.3 copy-start.9
  943.0 4.3 copy-start.10
  951.3 4.5 copy-start.4
  965.1 223.4 %reduce-scatter.12.cloned.1.call-start = ((), (), s32[]{:S(2)}) async-start(), calls=%async_computation.16 | async-start | bytes 12582912 | tf_op jit(solution)/shard_map/reduce_scatter | solution.py:243
  1057.4 210.5 %reduce-scatter.8.cloned.1.call-start = ((), (), s32[]{:S(2)}) async-start(), calls=%async_computation.13 | async-start | bytes 12582912 | tf_op jit(solution)/shard_map/reduce_scatter | solution.py:155
  1061.2 11.4 copy-start.7
  1078.2 255.6 %reduce-scatter.16.cloned.1.call-start = ((), (), s32[]{:S(2)}) async-start(), calls=%async_computation.18 | async-start | bytes 2228224 | tf_op jit(solution)/shard_map/reduce_scatter | solution.py:267
  1084.2 338.2 %reduce-scatter.14.cloned.1.call-start = ((), (), s32[]{:S(2)}) async-start(), calls=%async_computation.17 | async-start | bytes 6684672 | tf_op jit(solution)/shard_map/reduce_scatter | solution.py:263
  1096.7 432.9 %reduce-scatter.18.cloned.1.call-start = ((), (), s32[]{:S(2)}) async-start(), calls=%async_computation.19 | async-start | bytes 8912896 | tf_op jit(solution)/shard_map/reduce_scatter | solution.py:264
  1111.7 525.6 %reduce-scatter.20.cloned.1.call-start = ((), (), s32[]{:S(2)}) async-start(), calls=%async_computation.20 | async-start | bytes 8912896 | tf_op jit(solution)/shard_map/reduce_scatter | solution.py:268
  1126.6 61.9 %copy-start.2 = (bf16[1024,1024]{1,0:T(8,128)(2,1)S(1)}, bf16[1024,1024]{1,0:T(8,128)(2,1)}, u32[]{:S(2)}) copy-start(bf16[1024,1024]{1,0:T(8,128)(2,1)} %param.18) | copy-start | bytes 6291460
  1126.6 61.9 %copy-start.13 = (f32[1024]{0:T(1024)S(1)}, f32[1024]{0:T(1024)}, u32[]{:S(2)}) copy-start(f32[1024]{0:T(1024)} %copy-done.12) | copy-start | bytes 12292
  1126.6 61.9 %copy-start.15 = (f32[1024]{0:T(1024)S(1)}, f32[1024]{0:T(1024)}, u32[]{:S(2)}) copy-start(f32[1024]{0:T(1024)} %copy-done.14) | copy-start | bytes 12292
  1126.6 61.9 %copy-start.17 = (f32[1024]{0:T(1024)S(1)}, f32[1024]{0:T(1024)}, u32[]{:S(2)}) copy-start(f32[1024]{0:T(1024)} %param.20) | copy-start | bytes 12292
  1126.6 61.9 %copy-start.19 = (f32[1024]{0:T(1024)S(1)}, f32[1024]{0:T(1024)}, u32[]{:S(2)}) copy-start(f32[1024]{0:T(1024)} %param.22) | copy-start | bytes 12292
  1188.5 79.4 %copy-start.23 = (f32[1024]{0:T(1024)S(1)}, f32[1024]{0:T(1024)}, u32[]{:S(2)}) copy-start(f32[1024]{0:T(1024)} %param.31) | copy-start | bytes 12292
  1188.5 79.4 %copy-start.24 = (f32[1024]{0:T(1024)S(1)}, f32[1024]{0:T(1024)}, u32[]{:S(2)}) copy-start(f32[1024]{0:T(1024)} %param.27) | copy-start | bytes 12292
  1316.3 321.6 %copy-start.25 = (f32[1024]{0:T(1024)}, f32[1024]{0:T(1024)S(1)}, u32[]{:S(2)}) copy-start(f32[1024]{0:T(1024)S(1)} %get-tuple-element.552) | copy-start | bytes 12292
  (11 other events, 28.3 us)
Sparse Core Ops, SparseCore 0:
  10.2 69.3 all-gather.8
  81.2 58.8 all-gather.16
  141.6 56.7 all-gather.6
  199.7 56.7 all-gather.10
  258.5 50.2 all-gather.12
  310.8 48.8 all-gather.14
  965.2 99.2 reduce-scatter.9
  1066.8 99.3 reduce-scatter.11
  1168.5 99.3 reduce-scatter.7
  1272.0 61.8 reduce-scatter.15
  1338.4 83.9 reduce-scatter.13
  1426.9 102.6 reduce-scatter.17
  1534.2 103.0 reduce-scatter.19
